TPU v7x, 16 devices: a whole 2x2x2 slice. The times are simulated.
16 devices in a mesh: data: 4 (over z, y), stage: 4 (over x, core).
Axes of the slice: x: 2, y: 2, z: 2, core: 2. Of those that a mesh axis runs over, the one named last changes fastest.
Arguments:
- w_first: float32 [4, 128, 512], P('stage')
- w_second: float32 [4, 512, 128], P('stage')
- mom_first: float32 [4, 128, 512], P('stage')
- mom_second: float32 [4, 512, 128], P('stage')
- vel_first: float32 [4, 128, 512], P('stage')
- vel_second: float32 [4, 512, 128], P('stage')
- grad_first: float32 [4, 128, 512], P('stage')
- grad_second: float32 [4, 512, 128], P('stage')
- embed_table: float32 [30528, 128], replicated
- mom_embed: float32 [30528, 128], replicated
- vel_embed: float32 [30528, 128], replicated
- grad_embed: float32 [30528, 128], replicated
- stage_acts: bfloat16 [4, 4096, 128], P('stage', 'data')
- last_tokens: int32 [4096], P('data')
- targets: int32 [4096], P('data')
- next_tokens: int32 [16, 4096], P(None, 'data')
- max_norm: float32 [1], replicated
Outputs:
- output 1: float32 [4, 128, 512], P('stage')
- output 2: float32 [4, 512, 128], P('stage')
- output 3: float32 [4, 128, 512], P('stage')
- output 4: float32 [4, 512, 128], P('stage')
- output 5: float32 [4, 128, 512], P('stage')
- output 6: float32 [4, 512, 128], P('stage')
- output 7: float32 [30528, 128], replicated
- output 8: float32 [30528, 128], replicated
- output 9: float32 [30528, 128], replicated
- output 10: bfloat16 [16, 4096, 128], P(None, 'data')
All inputs are finite; a program needn't handle non-finite values.
Results may differ from a plain program's by a relative error of at most 0.00627237.
Values are sent between devices in bfloat16 or wider.
A program may use at most 1 GiB of HBM per device.

v0:
```python
import math
import jax
import jax.numpy as jnp
from jax import lax
from jax.sharding import PartitionSpec as P

STEP_COUNT = 10
LEARN_RATE = 1e-3
ADAM_BETA1 = 0.9
ADAM_BETA2 = 0.95
ADAM_EPS = 1e-8
WEIGHT_DECAY = 0.1
CLIP_EPS = 1e-6


def block_forward(act_in, w_in, w_out):
    pre_act = jnp.dot(act_in, w_in, preferred_element_type=jnp.float32)
    hidden = jax.nn.gelu(pre_act).astype(jnp.bfloat16)
    mlp_out = jnp.dot(hidden, w_out, preferred_element_type=jnp.float32)
    return (act_in.astype(jnp.float32) + mlp_out).astype(jnp.bfloat16)


def block_backward(d_out, act_in, w_in, w_out):
    pre_act = jnp.dot(act_in, w_in, preferred_element_type=jnp.float32)
    hidden, gelu_back = jax.vjp(jax.nn.gelu, pre_act)
    grad_out = jnp.einsum('tf,td->fd', hidden.astype(jnp.bfloat16), d_out, preferred_element_type=jnp.float32)
    d_hidden = jnp.einsum('td,fd->tf', d_out, w_out, preferred_element_type=jnp.float32)
    d_pre = gelu_back(d_hidden)[0].astype(jnp.bfloat16)
    grad_in = jnp.einsum('td,tf->df', act_in, d_pre, preferred_element_type=jnp.float32)
    d_back = jnp.einsum('tf,df->td', d_pre, w_in, preferred_element_type=jnp.float32)
    d_act = (d_out.astype(jnp.float32) + d_back).astype(jnp.bfloat16)
    return d_act, grad_in, grad_out


def head_backward(top_out, table_b, targets):
    logits = jnp.einsum('td,vd->tv', top_out, table_b, preferred_element_type=jnp.float32)
    soft_probs = jax.nn.softmax(logits, axis=-1)
    is_target = jnp.arange(table_b.shape[0])[None, :] == targets[:, None]
    d_logits = jnp.where(is_target, soft_probs - 1.0, soft_probs).astype(jnp.bfloat16)
    d_top = jnp.dot(d_logits, table_b, preferred_element_type=jnp.float32).astype(jnp.bfloat16)
    head_grad = jnp.einsum('tv,td->vd', d_logits, top_out, preferred_element_type=jnp.float32)
    return d_top, head_grad


def adamw_update(master, moment, velocity, gradient, clip_scale):
    scaled_grad = clip_scale * gradient
    moment_new = ADAM_BETA1 * moment + (1.0 - ADAM_BETA1) * scaled_grad
    velocity_new = ADAM_BETA2 * velocity + (1.0 - ADAM_BETA2) * scaled_grad * scaled_grad
    moment_hat = moment_new / (1.0 - ADAM_BETA1 ** STEP_COUNT)
    velocity_hat = velocity_new / (1.0 - ADAM_BETA2 ** STEP_COUNT)
    master_new = master - LEARN_RATE * (moment_hat / (jnp.sqrt(velocity_hat) + ADAM_EPS) + WEIGHT_DECAY * master)
    return master_new, moment_new, velocity_new


def solution(mesh):
    n_stage = mesh.shape['stage']
    n_rep = mesh.shape['data']
    down_pairs = [(j, j - 1) for j in range(1, n_stage)]
    up_pairs = [(j, j + 1) for j in range(n_stage - 1)]
    w_spec = P('stage', None, None)
    in_specs = (w_spec,) * 8 + (P(None, None),) * 4 + (P('stage', 'data', None), P('data'), P('data'), P(None, 'data'), P(None))
    out_specs = (w_spec,) * 6 + (P(None, None),) * 3 + (P(None, 'data', None),)

    def local_step(w_first, w_second, mom_first, mom_second, vel_first, vel_second, grad_first, grad_second,
                   embed_table, mom_embed, vel_embed, grad_embed, stage_acts, last_tokens, targets, next_tokens, max_norm):
        stage_id = lax.axis_index('stage')
        is_last = stage_id == n_stage - 1
        vocab, d_model = embed_table.shape
        scale_in = math.sqrt(d_model)
        w_in = w_first[0].astype(jnp.bfloat16)
        w_out = w_second[0].astype(jnp.bfloat16)
        table_b = embed_table.astype(jnp.bfloat16)
        act_in = stage_acts[0]

        def with_head(top_in):
            return head_backward(block_forward(top_in, w_in, w_out), table_b, targets)

        def without_head(top_in):
            return jnp.zeros_like(top_in), jnp.zeros((vocab, d_model), jnp.float32)

        d_top, head_grad = lax.cond(is_last, with_head, without_head, act_in)

        def back_step(step_idx, loop_state):
            d_in, sum_in, sum_out, d_keep = loop_state
            active = stage_id == n_stage - 1 - step_idx

            def work(operands):
                return block_backward(operands[0], act_in, w_in, w_out)

            def rest(operands):
                return jnp.zeros_like(operands[0]), operands[1], operands[2]

            d_act, sum_in, sum_out = lax.cond(active, work, rest, (d_in, sum_in, sum_out))
            d_keep = jnp.where(active, d_act, d_keep)
            d_in = lax.ppermute(d_act, 'stage', down_pairs)
            return d_in, sum_in, sum_out, d_keep

        init_state = (d_top, jnp.zeros(w_in.shape, jnp.float32), jnp.zeros(w_out.shape, jnp.float32), jnp.zeros_like(act_in))
        _, step_in, step_out, d_own = lax.fori_loop(0, n_stage, back_step, init_state)
        d_low = jnp.where(stage_id == 0, d_own, jnp.zeros_like(d_own))
        low_grad = scale_in * jax.ops.segment_sum(d_low.astype(jnp.float32), last_tokens, num_segments=vocab)

        full_first = grad_first[0] + lax.psum(step_in, 'data') / n_rep
        full_second = grad_second[0] + lax.psum(step_out, 'data') / n_rep
        full_embed = grad_embed + lax.psum(head_grad + low_grad, ('data', 'stage')) / n_rep
        stage_sq = jnp.sum(full_first * full_first) + jnp.sum(full_second * full_second)
        total_sq = lax.psum(stage_sq, 'stage') + jnp.sum(full_embed * full_embed)
        clip_scale = jnp.minimum(1.0, max_norm[0] / (jnp.sqrt(total_sq) + CLIP_EPS))
        new_first, new_mom_first, new_vel_first = adamw_update(w_first[0], mom_first[0], vel_first[0], full_first, clip_scale)
        new_second, new_mom_second, new_vel_second = adamw_update(w_second[0], mom_second[0], vel_second[0], full_second, clip_scale)
        new_embed, new_mom_embed, new_vel_embed = adamw_update(embed_table, mom_embed, vel_embed, full_embed, clip_scale)

        next_in = new_first.astype(jnp.bfloat16)
        next_out = new_second.astype(jnp.bfloat16)
        next_table = new_embed.astype(jnp.bfloat16)
        n_micro, tokens = next_tokens.shape
        start_act = (scale_in * jnp.take(next_table, next_tokens.reshape(-1), axis=0).astype(jnp.float32)).astype(jnp.bfloat16)

        def run_block(carry_act):
            return block_forward(carry_act, next_in, next_out)

        def keep_block(carry_act):
            return carry_act

        def fwd_step(step_idx, carry_act):
            carry_act = lax.cond(stage_id == step_idx, run_block, keep_block, carry_act)
            return lax.ppermute(carry_act, 'stage', up_pairs)

        carry_act = lax.fori_loop(0, n_stage - 1, fwd_step, start_act)
        final_act = lax.cond(is_last, run_block, keep_block, carry_act)
        gathered_out = lax.psum(jnp.where(is_last, final_act, jnp.zeros_like(final_act)), 'stage')
        next_acts = gathered_out.reshape(n_micro, tokens, d_model)
        return (new_first[None], new_second[None], new_mom_first[None], new_mom_second[None],
                new_vel_first[None], new_vel_second[None], new_embed, new_mom_embed, new_vel_embed, next_acts)

    return jax.shard_map(local_step, mesh=mesh, in_specs=in_specs, out_specs=out_specs, check_vma=False)
```

profile of v0, /device:TPU:0, one launch (start us, length us, event | category | flops | bytes accessed | tf_op | source)
XLA Modules:
  0.0 916.6 jit_solution(15993219779650799755)
XLA Ops:
  7.3 1.0 bitcast_convert_fusion
  8.3 1.7 bitcast_convert_fusion.1
  9.9 8.4 convert_element_type.93
  18.3 13.4 %conditional.4 = (bf16[1024,128]{1,0:T(8,128)(2,1)}, f32[30528,128]{1,0:T(8,128)}) conditional(s32[]{:T(128)} %convert_element_type.90, () %tuple.68, (s32[1024]{0:T(1024)S(1)}, bf16[1024,128]{1,0:T(8,128)(2,1)S(1)}, bf16[128,512]{1,0:T(8,128)(2,1)}, bf16[512,128]{1,0:T(8,128)(2,1)S(1)}, bf16[30528,128]{1,0:T(8,128)(2,1)}) %tuple.142), branch_computations={%region_0.0_spmd, %region_1.4_spmd} | conditional | flops 24563218432 | bytes 595550208 | solution.py:81
  18.3 5.9 broadcast.100
  31.8 238.2 %while.40 = (s32[]{:T(128)}, bf16[1024,128]{1,0:T(8,128)(2,1)}, f32[128,512]{0,1:T(8,128)S(1)}, f32[512,128]{1,0:T(8,128)S(1)}, bf16[1024,128]{1,0:T(8,128)(2,1)...) while((s32[]{:T(128)}, bf16[1024,128]{1,0:T(8,128)(2,1)}, ...), condition=%wide.region_7.8_spmd.clone, body=%wide.region_4.7_spmd.clone.sunk | while | flops 686948352 | bytes 13762826 | solution.py:99
  31.9 1.3 collective-permute-start.1
  33.3 2.3 collective-permute-done.1
  35.6 1.3 collective-permute-start.1
  37.0 7.2 collective-permute-done.1
  44.2 1.3 collective-permute-start.1
  45.6 213.5 %collective-permute-done.1 = bf16[1024,128]{1,0:T(8,128)(2,1)} collective-permute-done((bf16[1024,128]{1,0:T(8,128)(2,1)S(1)}, bf16[1024,128]{1,0:T(8,128)(2,1)}, u32[]{:S(2)}, u32[]{:S(2)}) %collective-permute-start.1) | collective-permute-done | bytes 262176 | tf_op jit(solution)/shard_map/while/body/eval_jaxpr/ppermute | solution.py:95
  259.1 7.6 conditional.10
  259.1 1.3 fusion.82
  260.4 2.5 fusion.27
  262.9 1.5 fusion.28
  264.9 1.8 fusion.29
  266.7 1.3 collective-permute-start.1
  268.0 2.0 collective-permute-done.1
  271.0 12.9 %scatter_custom_fusion = f32[30528,128]{1,0:T(8,128)} fusion(s32[1024]{0:T(1024)} %param.42, f32[]{:T(128)} %constant.92.clone.1, bf16[1024,128]{1,0:T(8,128)(2,1)S(1)} %get-tuple-element.336, pred[]{:T(512)S(6)} %eq.34, bf16[]{:T(256)} %constant.93.clone.1), kind=kCustom, calls=%fused_computation.85 | custom fusion | flops 393216 | bytes 15893505 | tf_op jit(solution)/shard_map/scatter-add | solution.py:101
  283.9 16.7 %multiply_add_fusion.2 = f32[30528,128]{1,0:T(8,128)} fusion(f32[30528,128]{1,0:T(8,128)} %get-tuple-element.335, f32[30528,128]{1,0:T(8,128)} %scatter_custom_fusion), kind=kLoop, calls=%fused_computation.83 | loop fusion | flops 7815168 | bytes 46891008 | tf_op jit(solution)/shard_map/add | solution.py:105
  301.7 8.2 all-reduce.9.cloned.1.call-done
  309.9 1.6 multiply_reduce_fusion.1
  311.6 1.6 multiply_reduce_fusion.2
  315.1 6.9 psum.37
  322.1 164.0 %all-reduce.5.cloned.1.call-done = f32[30528,128]{1,0:T(8,128)} async-done(((f32[30528,128]{1,0:T(8,128)}), f32[30528,128]{1,0:T(8,128)}) %all-reduce.5.cloned.1.call-update) | async-done | bytes 15630352 | tf_op jit(solution)/shard_map/psum | solution.py:105
  486.0 11.8 %multiply_reduce_fusion = f32[]{:T(128)} fusion(f32[30528,128]{1,0:T(8,128)} %param.40, f32[30528,128]{1,0:T(8,128)} %all-reduce.5.cloned.1.call-done), kind=kLoop, calls=%fused_computation.81 | loop fusion | flops 15630335 | bytes 31260676 | tf_op jit(solution)/shard_map/reduce_sum | solution.py:107
  499.2 45.7 %fusion.79 = (bf16[30528,128]{1,0:T(8,128)(2,1)}, f32[30528,128]{1,0:T(8,128)}, f32[30528,128]{1,0:T(8,128)}, f32[30528,128]{1,0:T(8,128)}) fusion(f32[30528,128]{1,0:T(8,128)} %param.37, f32[30528,128]{1,0:T(8,128)} %param.40, f32[30528,128]{1,0:T(8,128)} %all-reduce.5.cloned.1.call-done, f32[]{:T(128)S(6)} %min.3, f32[30528,128]{1,0:T(8,128)} %param.38, ...), kind=kLoop, calls=%fused_computation.122 | loop fusion | flops 74244096 | bytes 132857856 | tf_op jit(solution)/shard_map/convert_element_type | solution.py:115
  545.0 59.9 %gather_fusion = bf16[16384,128]{1,0:T(8,128)(2,1)} fusion(bf16[30528,128]{1,0:T(8,128)(2,1)} %get-tuple-element.407, s32[16384]{0:T(1024)S(1)} %broadcast_clamp_fusion), kind=kCustom, calls=%fused_computation | custom fusion | bytes 8454144 | tf_op jit(solution)/shard_map/jit(_take)/gather | solution.py:117
  604.9 11.5 %multiply_convert_fusion.2 = bf16[16384,128]{1,0:T(8,128)(2,1)} fusion(bf16[16384,128]{1,0:T(8,128)(2,1)} %gather_fusion, pred[16384]{0:T(1024)(128)(4,1)S(1)} %compare_and_fusion), kind=kLoop, calls=%fused_computation.84 | loop fusion | flops 8388608 | bytes 8404992 | tf_op jit(solution)/shard_map/convert_element_type | solution.py:117
  616.4 1.0 fusion.77
  617.4 1.0 fusion.78
  618.4 138.5 %while.39 = (s32[]{:T(128)}, bf16[16384,128]{1,0:T(8,128)(2,1)}, s32[]{:T(128)}, bf16[128,512]{1,0:T(8,128)(2,1)S(1)}, bf16[512,128]{1,0:T(8,128)(2,1)S(1)}, /*index=5*/s32[]{:T(128)}) while((s32[]{:T(128)}, bf16[16384,128]{1,0:T(8,128)(2,1)}, s32[]{:T(128)}, bf16[128,512]{1,0:T(8,128)(2,1)S(1)}, bf16[512,128]{1,0:T(8,128)(2,1)S(1)}, ...), condition=%wide.region_19.20_spmd, body=%wide.region_16.19_spmd.sunk | while | flops 4376756224 | bytes 42205336 | solution.py:129
  618.7 22.2 %conditional.9 = (bf16[16384,128]{1,0:T(8,128)(2,1)}) conditional(s32[]{:T(128)} %convert_element_type.138, bf16[16384,128]{1,0:T(8,128)(2,1)} %get-tuple-element.566, (bf16[16384,128]{1,0:T(8,128)(2,1)}, bf16[128,512]{1,0:T(8,128)(2,1)S(1)}, bf16[512,128]{1,0:T(8,128)(2,1)S(1)}) %tuple.110), branch_computations={%region_17.17_spmd, %region_18.18_spmd} | conditional | flops 4376756224 | bytes 17039368 | solution.py:126
  618.7 3.7 copy.70
  622.4 18.4 %fusion.42 = bf16[16384,128]{1,0:T(8,128)(2,1)} fusion(bf16[512,128]{1,0:T(8,128)(2,1)S(1)} %get-tuple-element.306, bf16[16384,128]{1,0:T(8,128)(2,1)} %copy.70, bf16[128,512]{1,0:T(8,128)(2,1)S(1)} %get-tuple-element.305), kind=kOutput, calls=%fused_computation.56 | convolution fusion | flops 4376756224 | bytes 8650752 | tf_op jit(solution)/shard_map/while/body/eval_jaxpr/cond/branch_1_fun/dot_general | solution.py:19
  640.8 3.2 collective-permute-start
  644.1 4.8 collective-permute-done
  648.9 3.7 copy.66
  652.6 44.7 %collective-permute-start = (bf16[16384,128]{1,0:T(8,128)(2,1)}, bf16[16384,128]{1,0:T(8,128)(2,1)}, u32[]{:S(2)}, u32[]{:S(2)}) collective-permute-start(bf16[16384,128]{1,0:T(8,128)(2,1)} %get-tuple-element.590), channel_id=1, source_target_pairs={{0,1},{1,2},{2,3},{4,5},{5,6},{6,7},{8,9},{9,10},{10,11},{12,13},{... | collective-permute-start | bytes 12582920 | tf_op jit(solution)/shard_map/while/body/eval_jaxpr/ppermute | solution.py:127
  697.3 4.8 collective-permute-done
  702.1 3.7 copy.66
  705.9 42.5 %collective-permute-start = (bf16[16384,128]{1,0:T(8,128)(2,1)}, bf16[16384,128]{1,0:T(8,128)(2,1)}, u32[]{:S(2)}, u32[]{:S(2)}) collective-permute-start(bf16[16384,128]{1,0:T(8,128)(2,1)} %get-tuple-element.590), channel_id=1, source_target_pairs={{0,1},{1,2},{2,3},{4,5},{5,6},{6,7},{8,9},{9,10},{10,11},{12,13},{... | collective-permute-start | bytes 12582920 | tf_op jit(solution)/shard_map/while/body/eval_jaxpr/ppermute | solution.py:127
  748.4 4.8 collective-permute-done
  753.2 3.7 copy.66
  756.9 2.2 broadcast_select_fusion
  759.1 145.9 %all-reduce.7.cloned.1.call-done = bf16[16,1024,128]{2,1,0:T(8,128)(2,1)} async-done(((bf16[16,1024,128]{2,1,0:T(8,128)(2,1)}), bf16[16,1024,128]{2,1,0:T(8,128)(2,1)}) %all-reduce.7.cloned.1.call-update) | async-done | bytes 4194320 | tf_op jit(solution)/shard_map/psum | solution.py:131
  905.0 4.6 copy.76
  (58 shorter events, 3.7 us)
Async XLA Ops:
  7.2 11.1 %copy-start = (bf16[1,1024,128]{2,1,0:T(8,128)(2,1)S(1)}, bf16[1,1024,128]{2,1,0:T(8,128)(2,1)}, u32[]{:S(2)}) copy-start(bf16[1,1024,128]{2,1,0:T(8,128)(2,1)} %param.41) | copy-start | bytes 786436
  7.2 11.1 %copy-start.13 = (s32[1024]{0:T(1024)S(1)}, s32[1024]{0:T(1024)}, u32[]{:S(2)}) copy-start(s32[1024]{0:T(1024)} %param.43) | copy-start | bytes 12292
  7.2 302.7 %all-reduce.9.cloned.1.call-start = ((), (), s32[]{:S(2)}) async-start(), calls=%async_computation.2 | async-start | bytes 1048576 | tf_op jit(solution)/shard_map/psum | solution.py:103
  8.2 10.1 %copy-start.12 = (bf16[512,128]{1,0:T(8,128)(2,1)}, bf16[512,128]{1,0:T(8,128)(2,1)S(1)}, u32[]{:S(2)}) copy-start(bf16[512,128]{1,0:T(8,128)(2,1)S(1)} %bitcast_convert_fusion) | copy-start | bytes 393220
  18.3 13.5 %copy-start.1 = (bf16[1024,128]{1,0:T(8,128)(2,1)S(1)}, bf16[1024,128]{1,0:T(8,128)(2,1)}, u32[]{:S(2)}) copy-start(bf16[1024,128]{1,0:T(8,128)(2,1)} %custom-call) | copy-start | bytes 786436
  31.9 3.6 collective-permute-start.1
  35.6 8.6 collective-permute-start.1
  44.2 214.9 %collective-permute-start.1 = (bf16[1024,128]{1,0:T(8,128)(2,1)S(1)}, bf16[1024,128]{1,0:T(8,128)(2,1)}, u32[]{:S(2)}, u32[]{:S(2)}) collective-permute-start(bf16[1024,128]{1,0:T(8,128)(2,1)S(1)} %get-tuple-element.510), channel_id=1, source_target_pairs={{1,0},{2,1},{3,2},{5,4},{6,5},{7,6},{9,8},{10,9},{11,10},{13,12},{... | collective-permute-start | bytes 786440 | tf_op jit(solution)/shard_map/while/body/eval_jaxpr/ppermute | solution.py:95
  266.7 3.4 collective-permute-start.1
  270.0 0.8 copy-start.4
  270.9 215.1 %all-reduce.5.cloned.1.call-start = ((), (), s32[]{:S(2)}) async-start(), calls=%async_computation | async-start | bytes 31260672 | tf_op jit(solution)/shard_map/psum | solution.py:105
  300.6 0.8 copy-start.9
  300.6 9.3 %copy-start.10 = (f32[1,512,128]{2,1,0:T(8,128)S(1)}, f32[1,512,128]{2,1,0:T(8,128)}, u32[]{:S(2)}) copy-start(f32[1,512,128]{2,1,0:T(8,128)} %param.36) | copy-start | bytes 786436
  300.6 10.9 %copy-start.11 = (f32[1,128,512]{2,1,0:T(8,128)S(1)}, f32[1,128,512]{2,1,0:T(8,128)}, u32[]{:S(2)}) copy-start(f32[1,128,512]{2,1,0:T(8,128)} %param.35) | copy-start | bytes 786436
  300.7 604.4 %all-reduce.7.cloned.1.call-start = ((), (), s32[]{:S(2)}) async-start(), calls=%async_computation.1 | async-start | bytes 8388608 | tf_op jit(solution)/shard_map/psum | solution.py:131
  544.9 71.5 %copy-start.2 = (f32[1,512,128]{2,1,0:T(8,128)S(1)}, f32[1,512,128]{2,1,0:T(8,128)}, u32[]{:S(2)}) copy-start(f32[1,512,128]{2,1,0:T(8,128)} %param.30) | copy-start | bytes 786436
  544.9 71.5 %copy-start.5 = (f32[1,512,128]{2,1,0:T(8,128)S(1)}, f32[1,512,128]{2,1,0:T(8,128)}, u32[]{:S(2)}) copy-start(f32[1,512,128]{2,1,0:T(8,128)} %param.34) | copy-start | bytes 786436
  545.0 71.5 %copy-start.6 = (f32[1,512,128]{2,1,0:T(8,128)S(1)}, f32[1,512,128]{2,1,0:T(8,128)}, u32[]{:S(2)}) copy-start(f32[1,512,128]{2,1,0:T(8,128)} %param.32) | copy-start | bytes 786436
  545.0 72.5 %copy-start.3 = (f32[1,128,512]{2,1,0:T(8,128)S(1)}, f32[1,128,512]{2,1,0:T(8,128)}, u32[]{:S(2)}) copy-start(f32[1,128,512]{2,1,0:T(8,128)} %param.29) | copy-start | bytes 786436
  545.0 72.5 %copy-start.7 = (f32[1,128,512]{2,1,0:T(8,128)S(1)}, f32[1,128,512]{2,1,0:T(8,128)}, u32[]{:S(2)}) copy-start(f32[1,128,512]{2,1,0:T(8,128)} %param.33) | copy-start | bytes 786436
  545.0 72.4 %copy-start.8 = (f32[1,128,512]{2,1,0:T(8,128)S(1)}, f32[1,128,512]{2,1,0:T(8,128)}, u32[]{:S(2)}) copy-start(f32[1,128,512]{2,1,0:T(8,128)} %param.31) | copy-start | bytes 786436
  640.8 8.1 collective-permute-start
  652.6 49.5 %collective-permute-start = (bf16[16384,128]{1,0:T(8,128)(2,1)}, bf16[16384,128]{1,0:T(8,128)(2,1)}, u32[]{:S(2)}, u32[]{:S(2)}) collective-permute-start(bf16[16384,128]{1,0:T(8,128)(2,1)} %get-tuple-element.590), channel_id=1, source_target_pairs={{0,1},{1,2},{2,3},{4,5},{5,6},{6,7},{8,9},{9,10},{10,11},{12,13},{... | collective-permute-start | bytes 12582920 | tf_op jit(solution)/shard_map/while/body/eval_jaxpr/ppermute | solution.py:127
  705.9 47.3 %collective-permute-start = (bf16[16384,128]{1,0:T(8,128)(2,1)}, bf16[16384,128]{1,0:T(8,128)(2,1)}, u32[]{:S(2)}, u32[]{:S(2)}) collective-permute-start(bf16[16384,128]{1,0:T(8,128)(2,1)} %get-tuple-element.590), channel_id=1, source_target_pairs={{0,1},{1,2},{2,3},{4,5},{5,6},{6,7},{8,9},{9,10},{10,11},{12,13},{... | collective-permute-start | bytes 12582920 | tf_op jit(solution)/shard_map/while/body/eval_jaxpr/ppermute | solution.py:127
Sparse Core Ops, SparseCore 0:
  271.0 38.8 all-reduce.8
  315.6 170.4 all-reduce.4
  759.2 145.7 all-reduce.6
where the time goes:
time: 925 us; the launch traced here: 917 us
  waiting for transfers between devices  558 us (60%)
  other arithmetic  117 us (13%)
  starting transfers between devices  95.7 us (10%)
  local copies, waits for them, and re-layouts  88 us (10%)
  matrix products  26 us (3%)
  between operations  17.7 us (2%)
    ppermute x4, waiting for transfers between devices, back_step(): d_in = lax.ppermute(d_act, 'stage', down_pairs)  225 us
    psum x1, waiting for transfers between devices, local_step(): lax.psum(head_grad + low_grad, ('data', 'stage')) / n_rep  164 us
    psum x1, waiting for transfers between devices, local_step(): lax.psum(jnp.where(is_last, final_act, jnp.zeros_like(final_act)), 'stage')  146 us
    ppermute x3, starting transfers between devices, fwd_step(): return lax.ppermute(carry_act, 'stage', up_pairs)  90.4 us
    gather x1, local copies, waits for them, and re-layouts, local_step(): jnp.take(next_table, next_tokens.reshape(-1), axis=0).astype(jnp.float32)  59.9 us
    convert_element_type x1, other arithmetic, local_step(): next_table = new_embed.astype(jnp.bfloat16)  45.7 us
  transfers between devices with their start and end apart: 10, of which 10 were waited for; matrix products, arithmetic and copies ran while one was open for 4% of the time, Pallas kernels for 0%

commit v1 on v0

v1 whole, which is shorter than its diff:
```python
import functools
import math
import jax
import jax.numpy as jnp
from jax import lax
from jax.experimental import pallas as pl
from jax.experimental.pallas import tpu as pltpu
from jax.sharding import PartitionSpec as P

STEP_COUNT = 10
LEARN_RATE = 1e-3
ADAM_BETA1 = 0.9
ADAM_BETA2 = 0.95
ADAM_EPS = 1e-8
WEIGHT_DECAY = 0.1
CLIP_EPS = 1e-6
GELU_A = math.sqrt(2.0 / math.pi)
GELU_B = 0.044715

MESH = pl.DeviceIdType.MESH
F32 = jnp.float32
BF16 = jnp.bfloat16
VOCAB = 30528
D = 128
FF = 512
TOK = 1024
CHUNK = 256
SHARD = 1920
N_SHARD = 16
N_DEV = 16
VPAD = SHARD * N_SHARD
ANY = pl.BlockSpec(memory_space=pl.ANY)
VMEM = pl.BlockSpec(memory_space=pltpu.VMEM)
SMEM = pl.BlockSpec(memory_space=pltpu.SMEM)


def dot(a, b):
    return jnp.dot(a, b, preferred_element_type=F32)


def dot_nt(a, b):
    return lax.dot_general(a, b, (((1,), (1,)), ((), ())), preferred_element_type=F32)


def dot_tn(a, b):
    return lax.dot_general(a, b, (((0,), (0,)), ((), ())), preferred_element_type=F32)


def gelu(x):
    return x * (0.5 * (1.0 + jnp.tanh(x * (GELU_A + (GELU_A * GELU_B) * (x * x)))))


def block_forward(act_in, w_in, w_out):
    hidden = gelu(dot(act_in, w_in)).astype(BF16)
    return (act_in.astype(F32) + dot(hidden, w_out)).astype(BF16)


def group_peer(group, me, shift, n):
    slot = lax.rem(me + shift, n)
    if group == 'all':
        return slot, {'data': slot // 4, 'stage': lax.rem(slot, 4)}
    return slot, {group: slot}


def group_me(group):
    if group == 'all':
        return lax.axis_index('data') * 4 + lax.axis_index('stage'), N_DEV
    return lax.axis_index(group), 4


def exchange_kernel(items, *refs):
    n_items = len(items)
    ins, outs = refs[:n_items], refs[n_items:2 * n_items]
    send_sem, recv_sem, local_sem = refs[2 * n_items:]
    groups = sorted({g for g, _ in items})
    if 'all' in groups:
        greet = ['all']
    else:
        greet = groups
    barrier = pltpu.get_barrier_semaphore()
    count = 0
    for g in greet:
        me, n = group_me(g)
        for k in range(1, n):
            _, dev = group_peer(g, me, k, n)
            pl.semaphore_signal(barrier, inc=1, device_id=dev, device_id_type=MESH)
            count += 1
    pl.semaphore_wait(barrier, count)
    copies = []
    base = 0
    for i, (g, mode) in enumerate(items):
        me, n = group_me(g)
        for k in range(1, n):
            slot, dev = group_peer(g, me, k, n)
            src = ins[i] if mode == 'gather' else ins[i].at[slot]
            cp = pltpu.make_async_remote_copy(
                src_ref=src, dst_ref=outs[i].at[me], send_sem=send_sem.at[base], recv_sem=recv_sem.at[base],
                device_id=dev, device_id_type=MESH)
            cp.start()
            copies.append((cp, i, k, base))
            base += 1
    locs = []
    for i, (g, mode) in enumerate(items):
        me, n = group_me(g)
        src = ins[i] if mode == 'gather' else ins[i].at[me]
        cp = pltpu.make_async_copy(src, outs[i].at[me], local_sem.at[i])
        cp.start()
        locs.append(cp)
    for cp, i, k, b in copies:
        cp.wait_send()
        g, mode = items[i]
        me, n = group_me(g)
        frm = lax.rem(me + n - k, n)
        _, dev = group_peer(g, me, n - k, n)
        src = ins[i] if mode == 'gather' else ins[i].at[frm]
        pltpu.make_async_remote_copy(
            src_ref=src, dst_ref=outs[i].at[frm], send_sem=send_sem.at[b], recv_sem=recv_sem.at[b],
            device_id=dev, device_id_type=MESH).wait_recv()
    for cp in locs:
        cp.wait()


def exchange(cid, *items):
    plan = tuple((g, m) for _, g, m in items)
    shapes, n_rem = [], 0
    for a, g, m in items:
        n = N_DEV if g == 'all' else 4
        chunk = a.shape if m == 'gather' else a.shape[1:]
        shapes.append(jax.ShapeDtypeStruct((n,) + tuple(chunk), a.dtype))
        n_rem += n - 1
    return pl.pallas_call(
        functools.partial(exchange_kernel, plan),
        out_shape=tuple(shapes),
        in_specs=[ANY] * len(items),
        out_specs=tuple([ANY] * len(items)),
        scratch_shapes=[pltpu.SemaphoreType.DMA((n_rem,)), pltpu.SemaphoreType.DMA((n_rem,)),
                        pltpu.SemaphoreType.DMA((len(items),))],
        compiler_params=pltpu.CompilerParams(collective_id=cid, has_side_effects=True),
        name=f'exchange_{cid}',
    )(*[a for a, _, _ in items])


def spread_kernel(z_ref, out_ref, send_sem, recv_sem, local_sem):
    stage = lax.axis_index('stage')
    barrier = pltpu.get_barrier_semaphore()
    for k in range(1, 4):
        pl.semaphore_signal(barrier, inc=1, device_id={'stage': lax.rem(stage + k, 4)}, device_id_type=MESH)
    pl.semaphore_wait(barrier, 3)

    @pl.when(stage == 3)
    def _():
        cps = []
        for p in range(3):
            cp = pltpu.make_async_remote_copy(
                src_ref=z_ref.at[p], dst_ref=out_ref, send_sem=send_sem.at[p], recv_sem=recv_sem,
                device_id={'stage': p}, device_id_type=MESH)
            cp.start()
            cps.append(cp)
        own = pltpu.make_async_copy(z_ref.at[3], out_ref, local_sem)
        own.start()
        own.wait()
        for cp in cps:
            cp.wait_send()

    @pl.when(stage != 3)
    def _():
        pltpu.make_async_remote_copy(
            src_ref=z_ref.at[0], dst_ref=out_ref, send_sem=send_sem.at[0], recv_sem=recv_sem,
            device_id={'stage': 3}, device_id_type=MESH).wait_recv()


def spread(cid, z):
    return pl.pallas_call(
        spread_kernel,
        out_shape=jax.ShapeDtypeStruct((CHUNK, D), BF16),
        in_specs=[ANY], out_specs=ANY,
        scratch_shapes=[pltpu.SemaphoreType.DMA((3,)), pltpu.SemaphoreType.DMA, pltpu.SemaphoreType.DMA],
        compiler_params=pltpu.CompilerParams(collective_id=cid, has_side_effects=True),
        name=f'spread_{cid}',
    )(z.reshape(4, CHUNK, D))


def swap_kernel(half_ref, out_ref, send_sem, recv_sem, local_sem):
    stage = lax.axis_index('stage')
    core = lax.rem(stage, 2)
    partner = stage + 1 - 2 * core
    barrier = pltpu.get_barrier_semaphore()
    pl.semaphore_signal(barrier, inc=1, device_id={'stage': partner}, device_id_type=MESH)
    pl.semaphore_wait(barrier, 1)
    cp = pltpu.make_async_remote_copy(
        src_ref=half_ref, dst_ref=out_ref.at[core], send_sem=send_sem, recv_sem=recv_sem,
        device_id={'stage': partner}, device_id_type=MESH)
    cp.start()
    own = pltpu.make_async_copy(half_ref, out_ref.at[core], local_sem)
    own.start()
    own.wait()
    cp.wait_send()
    pltpu.make_async_remote_copy(
        src_ref=half_ref, dst_ref=out_ref.at[1 - core], send_sem=send_sem, recv_sem=recv_sem,
        device_id={'stage': partner}, device_id_type=MESH).wait_recv()


def swap(cid, half):
    return pl.pallas_call(
        swap_kernel,
        out_shape=jax.ShapeDtypeStruct((2,) + half.shape, half.dtype),
        in_specs=[VMEM], out_specs=VMEM,
        scratch_shapes=[pltpu.SemaphoreType.DMA, pltpu.SemaphoreType.DMA, pltpu.SemaphoreType.DMA],
        compiler_params=pltpu.CompilerParams(collective_id=cid, has_side_effects=True),
        name=f'swap_{cid}',
    )(half)


def head1_kernel(z_ref, tgt_ref, e_ref, dz_ref, lse_ref, eb, ex, mt, run_m, run_s):
    t = pl.program_id(0)
    n = pl.num_programs(0)

    @pl.when(t == 0)
    def _():
        run_m[...] = jnp.full_like(run_m, -1e30)
        run_s[...] = jnp.zeros_like(run_s)

    row = lax.broadcasted_iota(jnp.int32, (SHARD, D), 0) + t * SHARD
    tile = jnp.where(row < VOCAB, e_ref[...], 0.0).astype(BF16)
    eb[t] = tile
    lane = lax.broadcasted_iota(jnp.int32, (1, 128), 1)

    def logits_part(j, carry):
        part = eb[t, pl.ds(j * 384, 384), :]
        logits = dot_nt(z_ref[...], part)
        old = run_m[...]
        new = old
        cols = []
        for c in range(3):
            ok = lane + (t * SHARD + j * 384 + c * 128) < VOCAB
            col = jnp.where(ok, logits[:, c * 128:(c + 1) * 128], -1e30)
            cols.append(col)
            new = jnp.maximum(new, col)
        total = run_s[...] * jnp.exp(old - new)
        for c in range(3):
            e = jnp.exp(cols[c] - new)
            total = total + e
            ex[t, :, pl.ds(pl.multiple_of(j * 384 + c * 128, 128), 128)] = e
        mt[t, j] = new
        run_m[...] = new
        run_s[...] = total
        return carry

    lax.fori_loop(0, 5, logits_part, 0)

    @pl.when(t == n - 1)
    def _():
        top = jnp.max(run_m[...], axis=1, keepdims=True)
        total = jnp.sum(run_s[...] * jnp.exp(run_m[...] - top), axis=1, keepdims=True)
        lse_ref[...] = jnp.broadcast_to(top + jnp.log(total), lse_ref.shape)
        inv = 1.0 / total
        run_m[...] = jnp.broadcast_to(top, run_m.shape)
        run_s[...] = jnp.broadcast_to(inv, run_s.shape)
        hit = tgt_ref[...] - lax.broadcasted_iota(jnp.int32, (CHUNK, 128), 1)

        def back_tile(i, acc):
            tt = i // 5
            j = i - tt * 5
            scale = jnp.exp(mt[tt, j] - run_m[...]) * run_s[...]
            cols = []
            for c in range(3):
                start = j * 384 + c * 128
                e = ex[tt, :, pl.ds(pl.multiple_of(start, 128), 128)] * scale
                cols.append(jnp.where(hit == tt * SHARD + start, e - 1.0, e).astype(BF16))
            return acc + dot(jnp.concatenate(cols, axis=1), eb[tt, pl.ds(pl.multiple_of(j * 384, 128), 384), :])

        acc = lax.fori_loop(0, N_SHARD * 5, back_tile, jnp.zeros((CHUNK, D), F32))
        dz_ref[...] = acc.astype(BF16)


def head1(z, tgt, table):
    return pl.pallas_call(
        head1_kernel,
        grid=(N_SHARD,),
        out_shape=(jax.ShapeDtypeStruct((CHUNK, D), BF16), jax.ShapeDtypeStruct((CHUNK, 128), F32)),
        in_specs=[pl.BlockSpec((CHUNK, D), lambda t: (0, 0)), pl.BlockSpec((CHUNK, 128), lambda t: (0, 0)),
                  pl.BlockSpec((SHARD, D), lambda t: (t, 0))],
        out_specs=(pl.BlockSpec((CHUNK, D), lambda t: (0, 0)), pl.BlockSpec((CHUNK, 128), lambda t: (0, 0))),
        scratch_shapes=[pltpu.VMEM((N_SHARD, SHARD, D), BF16), pltpu.VMEM((N_SHARD, CHUNK, SHARD), F32),
                        pltpu.VMEM((N_SHARD, 5, CHUNK, 128), F32),
                        pltpu.VMEM((CHUNK, 128), F32), pltpu.VMEM((CHUNK, 128), F32)],
        cost_estimate=pl.CostEstimate(flops=20_000_000_000, bytes_accessed=16_000_000, transcendentals=8_000_000),
        name='head_pass1',
    )(z, jnp.broadcast_to(tgt[:, None], (CHUNK, 128)), table)


P2_ROWS = 480
P2_TOK = 512


def head2_kernel(me_ref, e_ref, z_ref, lse_ref, tgt_ref, de_ref, eb):
    t = pl.program_id(0)
    base = me_ref[0] * SHARD

    @pl.when(t == 0)
    def _():
        row = lax.broadcasted_iota(jnp.int32, (SHARD, D), 0) + base
        eb[...] = jnp.where(row < VOCAB, e_ref[...], 0.0).astype(BF16)
        de_ref[...] = jnp.zeros_like(de_ref)

    z = z_ref[...]

    def part(j, carry):
        rows = pl.ds(pl.multiple_of(j * P2_ROWS, 16), P2_ROWS)
        logits = dot_nt(eb[rows, :], z)
        row = lax.broadcasted_iota(jnp.int32, (P2_ROWS, P2_TOK), 0) + (base + j * P2_ROWS)
        p = jnp.exp(logits - lse_ref[...])
        p = jnp.where(row == tgt_ref[...], p - 1.0, p).astype(BF16)
        de_ref[rows, :] += dot(p, z)
        return carry

    lax.fori_loop(0, SHARD // P2_ROWS, part, 0)

    @pl.when(t == pl.num_programs(0) - 1)
    def _():
        row = lax.broadcasted_iota(jnp.int32, (SHARD, D), 0) + base
        de_ref[...] = jnp.where(row < VOCAB, de_ref[...], 0.0)


def head2(me, table, z_all, lse, tgt):
    n_tok = z_all.shape[0]
    return pl.pallas_call(
        head2_kernel,
        grid_spec=pltpu.PrefetchScalarGridSpec(
            num_scalar_prefetch=1,
            grid=(n_tok // P2_TOK,),
            in_specs=[pl.BlockSpec((SHARD, D), lambda t, m: (m[0], 0)), pl.BlockSpec((P2_TOK, D), lambda t, m: (t, 0)),
                      pl.BlockSpec((1, P2_TOK), lambda t, m: (0, t)), pl.BlockSpec((1, P2_TOK), lambda t, m: (0, t))],
            out_specs=pl.BlockSpec((SHARD, D), lambda t, m: (0, 0)),
            scratch_shapes=[pltpu.VMEM((SHARD, D), BF16)]),
        out_shape=jax.ShapeDtypeStruct((SHARD, D), F32),
        cost_estimate=pl.CostEstimate(flops=10_000_000_000, bytes_accessed=4_000_000, transcendentals=8_000_000),
        name='head_pass2',
    )(me, table, z_all, lse.reshape(1, n_tok), tgt.reshape(1, n_tok))


def chain_kernel(st_ref, a_ref, g_ref, w1_ref, w2_ref, dl_ref, d1_ref, d2_ref):
    t = pl.program_id(0)

    @pl.when(t == 0)
    def _():
        d1_ref[...] = jnp.zeros_like(d1_ref)
        d2_ref[...] = jnp.zeros_like(d2_ref)

    def one(i, g):
        p = 3 - i
        a = a_ref[p]
        u = dot(a, w1_ref[p])
        sq = u * u
        th = jnp.tanh(u * (GELU_A + (GELU_A * GELU_B) * sq))
        cdf = 0.5 * (1.0 + th)
        slope = cdf + (0.5 * u) * (1.0 - th * th) * (GELU_A + (3.0 * GELU_A * GELU_B) * sq)
        s = (dot_nt(g, w2_ref[p]) * slope).astype(BF16)

        @pl.when(p == st_ref[0])
        def _():
            h = (u * cdf).astype(BF16)
            d2_ref[...] += dot_tn(h, g)
            d1_ref[...] += dot_tn(a, s)

        return (g.astype(F32) + dot_nt(s, w1_ref[p])).astype(BF16)

    dl_ref[...] = lax.fori_loop(0, 4, one, g_ref[...])


def chain(stage, acts, g, w1, w2):
    n = TOK // CHUNK
    return pl.pallas_call(
        chain_kernel,
        grid_spec=pltpu.PrefetchScalarGridSpec(
            num_scalar_prefetch=1,
            grid=(n,),
            in_specs=[pl.BlockSpec((4, CHUNK, D), lambda t, s: (0, t, 0)), pl.BlockSpec((CHUNK, D), lambda t, s: (t, 0)),
                      pl.BlockSpec((4, D, FF), lambda t, s: (0, 0, 0)), pl.BlockSpec((4, FF, D), lambda t, s: (0, 0, 0))],
            out_specs=(pl.BlockSpec((CHUNK, D), lambda t, s: (t, 0)), pl.BlockSpec((D, FF), lambda t, s: (0, 0)),
                       pl.BlockSpec((FF, D), lambda t, s: (0, 0)))),
        out_shape=(jax.ShapeDtypeStruct((TOK, D), BF16), jax.ShapeDtypeStruct((D, FF), F32),
                   jax.ShapeDtypeStruct((FF, D), F32)),
        cost_estimate=pl.CostEstimate(flops=5_000_000_000, bytes_accessed=4_000_000, transcendentals=2_000_000),
        name='back_chain',
    )(stage, acts, g, w1, w2)


ADD_PARTS = 16
ADD_ROWS = VOCAB // ADD_PARTS


def rows_kernel(me_ref, tok_ref, dl_ref, de_ref, g_hbm, base_hbm, sq_ref, acc, rows, in_sem, out_sem):
    n_tok = dl_ref.shape[0]
    ins = [pltpu.make_async_copy(g_hbm.at[pl.ds(k * ADD_ROWS, ADD_ROWS)], acc.at[pl.ds(k * ADD_ROWS, ADD_ROWS)], in_sem.at[k])
           for k in range(ADD_PARTS)]
    for cp in ins:
        cp.start()
    rows[...] = dl_ref[...].astype(F32) * (math.sqrt(D) / 4.0)
    for cp in ins:
        cp.wait()

    def add(i, carry):
        for j in range(8):
            r = i * 8 + j
            at = pl.ds(tok_ref[r], 1)
            acc[at, :] = acc[at, :] + rows[pl.ds(r, 1), :]
        return carry

    lax.fori_loop(0, n_tok // 8, add, 0)
    outs = [pltpu.make_async_copy(acc.at[pl.ds(k * ADD_ROWS, ADD_ROWS)], base_hbm.at[pl.ds(k * ADD_ROWS, ADD_ROWS)], out_sem.at[k])
            for k in range(ADD_PARTS)]
    for cp in outs:
        cp.start()
    base = me_ref[0] * SHARD
    row = lax.broadcasted_iota(jnp.int32, (64, D), 0)

    def square(k, total):
        at = pl.multiple_of(k * 64, 8)
        val = acc[pl.ds(pl.multiple_of(base + at, 8), 64), :] + 0.25 * de_ref[pl.ds(at, 64), :]
        val = jnp.where(row + (base + at) < VOCAB, val, 0.0)
        return total + val * val

    total = lax.fori_loop(0, SHARD // 64, square, jnp.zeros((64, D), F32))
    sq_ref[...] = jnp.full(sq_ref.shape, jnp.sum(total), F32)
    for cp in outs:
        cp.wait()


def add_rows(me, tokens, dl, de, gacc):
    return pl.pallas_call(
        rows_kernel,
        out_shape=(jax.ShapeDtypeStruct((VOCAB, D), F32), jax.ShapeDtypeStruct((8, 128), F32)),
        in_specs=[SMEM, SMEM, VMEM, VMEM, ANY],
        out_specs=(ANY, VMEM),
        scratch_shapes=[pltpu.VMEM((VPAD, D), F32), pltpu.VMEM((dl.shape[0], D), F32),
                        pltpu.SemaphoreType.DMA((ADD_PARTS,)), pltpu.SemaphoreType.DMA((ADD_PARTS,))],
        cost_estimate=pl.CostEstimate(flops=10_000_000_000, bytes_accessed=32_000_000, transcendentals=0),
        name='add_rows',
    )(me, tokens, dl, de, gacc)


def adamw_update(master, moment, velocity, gradient, clip_scale):
    g = clip_scale * gradient
    m = ADAM_BETA1 * moment + (1.0 - ADAM_BETA1) * g
    v = ADAM_BETA2 * velocity + (1.0 - ADAM_BETA2) * g * g
    m_hat = m * (1.0 / (1.0 - ADAM_BETA1 ** STEP_COUNT))
    v_hat = v * (1.0 / (1.0 - ADAM_BETA2 ** STEP_COUNT))
    w = master - LEARN_RATE * (m_hat / (jnp.sqrt(v_hat) + ADAM_EPS) + WEIGHT_DECAY * master)
    return w, m, v


def adam_kernel(c_ref, w_ref, m_ref, v_ref, b_ref, de_ref, w_out, m_out, v_out):
    w, m, v = adamw_update(w_ref[...], m_ref[...], v_ref[...], b_ref[...] + 0.25 * de_ref[...], c_ref[0])
    w_out[...] = w
    m_out[...] = m
    v_out[...] = v


def adam(c, w, m, v, base, de):
    spec = pl.BlockSpec((SHARD, D), lambda t: (t, 0))
    shape = jax.ShapeDtypeStruct((VOCAB, D), F32)
    return pl.pallas_call(
        adam_kernel,
        grid=(N_SHARD,),
        out_shape=(shape, shape, shape),
        in_specs=[SMEM] + [spec] * 5,
        out_specs=(spec, spec, spec),
        cost_estimate=pl.CostEstimate(flops=20_000_000_000, bytes_accessed=125_000_000, transcendentals=8_000_000),
        name='adam_embed',
    )(c.reshape(1), w, m, v, base, de)


FW_TOK = 512


def forward_kernel(tok_ref, table_hbm, w1_ref, w2_ref, out_ref, table, x, sem):
    t = pl.program_id(0)
    copies = [pltpu.make_async_copy(table_hbm.at[pl.ds(k * ADD_ROWS, ADD_ROWS)], table.at[pl.ds(k * ADD_ROWS, ADD_ROWS)], sem.at[k])
              for k in range(ADD_PARTS)]

    @pl.when(t == 0)
    def _():
        for cp in copies:
            cp.start()
        for cp in copies:
            cp.wait()

    def take(i, carry):
        for j in range(16):
            r = i * 16 + j
            x[pl.ds(r, 1), :] = table[pl.ds(tok_ref[t * FW_TOK + r], 1), :]
        return carry

    lax.fori_loop(0, FW_TOK // 16, take, 0)
    act = (math.sqrt(D) * x[...].astype(BF16).astype(F32)).astype(BF16)
    for p in range(4):
        act = block_forward(act, w1_ref[p], w2_ref[p])
    out_ref[...] = act


def forward(tokens, table, w1, w2):
    n = tokens.shape[0]
    return pl.pallas_call(
        forward_kernel,
        grid=(n // FW_TOK,),
        out_shape=jax.ShapeDtypeStruct((n, D), BF16),
        in_specs=[SMEM, ANY, pl.BlockSpec((4, D, FF), lambda t: (0, 0, 0)), pl.BlockSpec((4, FF, D), lambda t: (0, 0, 0))],
        out_specs=pl.BlockSpec((FW_TOK, D), lambda t: (t, 0)),
        scratch_shapes=[pltpu.VMEM((VOCAB, D), F32), pltpu.VMEM((FW_TOK, D), F32), pltpu.SemaphoreType.DMA((ADD_PARTS,))],
        name='forward',
    )(tokens, table, w1, w2)


def solution(mesh):
    w_spec = P('stage', None, None)
    in_specs = (w_spec,) * 8 + (P(None, None),) * 4 + (P('stage', 'data', None), P('data'), P('data'), P(None, 'data'), P(None))
    out_specs = (w_spec,) * 6 + (P(None, None),) * 3 + (P(None, 'data', None),)

    def local_step(w_first, w_second, mom_first, mom_second, vel_first, vel_second, grad_first, grad_second,
                   embed_table, mom_embed, vel_embed, grad_embed, stage_acts, last_tokens, targets, next_tokens, max_norm):
        stage = lax.axis_index('stage')
        data = lax.axis_index('data')
        me = (data * 4 + stage).reshape(1).astype(jnp.int32)
        w_in = w_first[0].astype(BF16)
        w_out = w_second[0].astype(BF16)
        acts = stage_acts[0]

        z_full = block_forward(acts, w_in, w_out)
        z = spread(0, z_full)
        z_all = lax.all_gather(z, ('data', 'stage'), tiled=True)
        acts_all = lax.all_gather(acts, 'stage')
        w1_all = lax.all_gather(w_in, 'stage')
        w2_all = lax.all_gather(w_out, 'stage')

        tgt = lax.dynamic_slice(targets, (stage * CHUNK,), (CHUNK,))
        dz, lse = head1(z, tgt, embed_table)
        lse_rows = lse[:, 0].reshape(2, 128)
        g, lse_all, tgt_all, tok_all = exchange(
            1, (dz, 'stage', 'gather'), (lse_rows, 'all', 'gather'),
            (targets.reshape(8, 128), 'data', 'gather'), (last_tokens.reshape(8, 128), 'data', 'gather'))
        de = head2(me, embed_table, z_all, lse_all, tgt_all)
        de_all = lax.all_gather(de, ('data', 'stage'), tiled=True)

        d_low, step_in, step_out = chain(stage.reshape(1).astype(jnp.int32), acts_all, g.reshape(TOK, D), w1_all, w2_all)
        dl_all, r1, r2 = exchange(
            2, (d_low, 'data', 'gather'), (step_in.reshape(4, D // 4, FF), 'data', 'scatter'),
            (step_out.reshape(4, FF // 4, D), 'data', 'scatter'))
        base, shard_sq = add_rows(me, tok_all.reshape(-1), dl_all.reshape(-1, D), de, grad_embed)
        part1 = lax.dynamic_slice(grad_first[0], (data * (D // 4), 0), (D // 4, FF)) + jnp.sum(r1, axis=0) * 0.25
        part2 = lax.dynamic_slice(grad_second[0], (data * (FF // 4), 0), (FF // 4, D)) + jnp.sum(r2, axis=0) * 0.25
        sq = shard_sq + (jnp.sum(part1 * part1) + jnp.sum(part2 * part2))
        sq_all, full1, full2 = exchange(3, (sq, 'all', 'gather'), (part1, 'data', 'gather'), (part2, 'data', 'gather'))
        total_sq = jnp.sum(sq_all[:, 0, 0])
        clip_scale = jnp.minimum(1.0, max_norm[0] / (jnp.sqrt(total_sq) + CLIP_EPS))

        new_first, new_mom_first, new_vel_first = adamw_update(
            w_first[0], mom_first[0], vel_first[0], full1.reshape(D, FF), clip_scale)
        new_second, new_mom_second, new_vel_second = adamw_update(
            w_second[0], mom_second[0], vel_second[0], full2.reshape(FF, D), clip_scale)
        n1_all = lax.all_gather(new_first.astype(BF16), 'stage')
        n2_all = lax.all_gather(new_second.astype(BF16), 'stage')
        new_embed, new_mom_embed, new_vel_embed = adam(clip_scale, embed_table, mom_embed, vel_embed, base, de_all)

        n_micro, tokens = next_tokens.shape
        core = lax.rem(stage, 2)
        mine = lax.dynamic_slice(next_tokens, (core * (n_micro // 2), 0), (n_micro // 2, tokens)).reshape(-1)
        half = forward(mine, new_embed, n1_all, n2_all)
        next_acts = swap(4, half).reshape(n_micro, tokens, D)
        return (new_first[None], new_second[None], new_mom_first[None], new_mom_second[None],
                new_vel_first[None], new_vel_second[None], new_embed, new_mom_embed, new_vel_embed, next_acts)

    return jax.shard_map(local_step, mesh=mesh, in_specs=in_specs, out_specs=out_specs, check_vma=False)
```

time: 925 us -> 336 us (0.36)
  waiting for transfers between devices: 558 us -> 0.75 us
  Pallas kernels: 0 us -> 261 us
  other arithmetic: 117 us -> 13.9 us
  starting transfers between devices: 95.7 us -> 0.12 us
  local copies, waits for them, and re-layouts: 88 us -> 8.42 us
  blocking collectives: 6.95 us -> 31.7 us
  matrix products: 26 us -> 2.68 us
    psum x3 -> x0, waiting for transfers between devices: 318 us -> none  [the longest x1 164 us: local_step(): lax.psum(head_grad + low_grad, ('data', 'stage')) / n_rep]
    pallas_call x0 -> x11, Pallas kernels: none -> 261 us  [the longest x1 49.1 us: forward(): pl.pallas_call(forward_kernel, grid=(n // FW_TOK,), out_shape=jax.ShapeDt...]
    ppermute x7 -> x0, waiting for transfers between devices: 239 us -> none  [the longest x4 225 us: back_step(): d_in = lax.ppermute(d_act, 'stage', down_pairs)]
    ppermute x7 -> x0, starting transfers between devices: 95.6 us -> none  [the longest x3 90.4 us: fwd_step(): return lax.ppermute(carry_act, 'stage', up_pairs)]
    convert_element_type x7 -> x4, other arithmetic: 70.3 us -> 3.95 us  [the longest x1 1.01 us: local_step(): n1_all = lax.all_gather(new_first.astype(BF16), 'stage')]
    gather x1 -> x0, local copies, waits for them, and re-layouts: 59.9 us -> none  [local_step(): jnp.take(next_table, next_tokens.reshape(-1), axis=0).astype(jnp.float32)]
    all_gather x0 -> x4, blocking collectives: none -> 31.7 us  [the longest x1 10.5 us: local_step(): w2_all = lax.all_gather(w_out, 'stage')]
    dot_general x6 -> x1, matrix products: 26 us -> 2.68 us  [dot(): return jnp.dot(a, b, preferred_element_type=F32)]
  transfers between devices with their start and end apart: 10 -> 3, of which waited for: 10 -> 0; matrix products, arithmetic and copies ran while one was open for 4% -> 5% of each run, Pallas kernels for 0% -> 46%
where the time goes in v1:
time: 336 us; the launch traced here: 335 us
  Pallas kernels  261 us (78%)
  blocking collectives  31.7 us (9%)
  between operations  16.7 us (5%)
  other arithmetic  13.9 us (4%)
  local copies, waits for them, and re-layouts  8.42 us (3%)
    pallas_call x1, Pallas kernels, forward(): pl.pallas_call(forward_kernel, grid=(n // FW_TOK,), out_shape=jax.ShapeDt...  49.1 us
    pallas_call x1, Pallas kernels, head1(): pl.pallas_call(head1_kernel, grid=(N_SHARD,), out_shape=(jax.ShapeDtypeSt...  46.8 us
    pallas_call x3, Pallas kernels, exchange(): pl.pallas_call(functools.partial(exchange_kernel, plan), out_shape=tuple(...  46.7 us
    pallas_call x1, Pallas kernels, adam(): pl.pallas_call(adam_kernel, grid=(N_SHARD,), out_shape=(shape, shape, sha...  46 us
    pallas_call x1, Pallas kernels, add_rows(): pl.pallas_call(rows_kernel, out_shape=(jax.ShapeDtypeStruct((VOCAB, D), F...  25.3 us
    pallas_call x1, Pallas kernels, head2(): pl.pallas_call(head2_kernel, grid_spec=pltpu.PrefetchScalarGridSpec(num_s...  19.4 us
    pallas_call x1, Pallas kernels, chain(): pl.pallas_call(chain_kernel, grid_spec=pltpu.PrefetchScalarGridSpec(num_s...  14.4 us
    all_gather x1, blocking collectives, local_step(): w2_all = lax.all_gather(w_out, 'stage')  10.5 us
  transfers between devices with their start and end apart: 3, of which 0 were waited for; matrix products, arithmetic and copies ran while one was open for 5% of the time, Pallas kernels for 46%

profile of v1, /device:TPU:0, one launch (start us, length us, event | category | flops | bytes accessed | tf_op | source)
XLA Modules:
  0.0 334.9 jit_solution(12118364550419411622)
XLA Ops:
  7.2 0.0 copy-start
  7.2 0.0 all-gather.6.cloned.1.call-start
  7.2 1.0 convert_element_type.32
  8.2 1.0 convert_element_type.35
  9.2 2.7 fusion.2
  11.9 5.3 %spread_0.1.z_ref = bf16[256,128]{1,0:T(8,128)(2,1)} custom-call(bf16[4,256,128]{2,1,0:T(8,128)(2,1)} %bitcast.58), custom_call_target="tpu_custom_call" | custom-call | tf_op jit(solution)/shard_map/spread_0/pallas_call | solution.py:173
  17.2 0.0 all-gather.6.cloned.1.call-update
  17.2 0.0 all-gather.4.cloned.1.call-start
  17.3 0.7 all-gather.4.cloned.1.call-update
  18.0 0.0 all-gather.8.cloned.1.call-start
  18.0 0.8 dynamic_slice.16
  18.8 0.8 broadcast_in_dim.2.tgt_ref
  19.6 46.8 %head_pass1.1 = (bf16[256,128]{1,0:T(8,128)(2,1)}, f32[256,128]{1,0:T(8,128)}) custom-call(bf16[256,128]{1,0:T(8,128)(2,1)} %spread_0.1.z_ref, s32[256,128]{1,0:T(8,128)} %broadcast_in_dim.2.tgt_ref, f32[30528,128]{1,0:T(8,128)} %w_ref.1), custom_call_target="tpu_custom_call" | custom-call | flops 20000000000 | bytes 16000000 | tf_op jit(solution)/shard_map/head_pass1/pallas_call | solution.py:277
  66.3 1.6 slice_reduce_fusion
  67.9 8.7 %exchange_1.1 = (bf16[4,256,128]{2,1,0:T(8,128)(2,1)}, f32[16,2,128]{2,1,0:T(2,128)}, s32[4,8,128]{2,1,0:T(8,128)}, s32[4,8,128]{2,1,0:T(8,128)}) custom-call(bf16[256,128]{1,0:T(8,128)(2,1)} %get-tuple-element.30.refs_0_, f32[2,128]{1,0:T(2,128)} %bitcast.61, s32[8,128]{1,0:T(8,128)} %bitcast.60, s32[8,128]{1,0:T(8,128)} %bitcast.62), custom_call_target="tpu_custom_call" | custom-call | tf_op jit(solution)/shard_map/exchange_1/pallas_call | solution.py:131
  76.7 0.0 all-gather.6.cloned.1.call-done.z_ref
  76.7 19.4 %head_pass2.1.de_ref = f32[1920,128]{1,0:T(8,128)} custom-call(s32[1]{0:T(128)} %bitcast.1.me_ref, f32[30528,128]{1,0:T(8,128)} %w_ref.1, bf16[4096,128]{1,0:T(8,128)(2,1)} %all-gather.6.cloned.1.call-done.z_ref, f32[1,4096]{1,0:T(1,128)} %bitcast.66, s32[1,4096]{1,0:T(1,128)} %bitcast.67), custom_call_target="tpu_custom_call" | custom-call | flops 10000000000 | bytes 4000000 | tf_op jit(solution)/shard_map/head_pass2/pallas_call | solution.py:327
  96.1 0.0 all-gather.8.cloned.1.call-update
  96.8 0.6 copy.29
  97.4 7.1 %all_gather.26.w1_ref = bf16[4,128,512]{2,1,0:T(8,128)(2,1)} all-gather(bf16[1,128,512]{2,1,0:T(8,128)(2,1)S(1)} %convert_element_type.32), channel_id=1, replica_groups=mesh['data'=4,'stage'=4] {'stage'}, dimensions={0}, use_global_device_ids=true | all-gather | bytes 655360 | tf_op jit(solution)/shard_map/all_gather | solution.py:533
  104.5 10.5 %all_gather.27.w2_ref = bf16[4,512,128]{2,1,0:T(8,128)(2,1)} all-gather(bf16[1,512,128]{2,1,0:T(8,128)(2,1)S(1)} %convert_element_type.35), channel_id=1, replica_groups=mesh['data'=4,'stage'=4] {'stage'}, dimensions={0}, use_global_device_ids=true | all-gather | bytes 655360 | tf_op jit(solution)/shard_map/all_gather | solution.py:534
  115.0 14.4 %back_chain.1 = (bf16[1024,128]{1,0:T(8,128)(2,1)}, f32[128,512]{1,0:T(8,128)}, f32[512,128]{1,0:T(8,128)}) custom-call(s32[1]{0:T(128)} %bitcast.9.st_ref, bf16[4,1024,128]{2,1,0:T(8,128)(2,1)} %all-gather.4.cloned.1.call-done.a_ref, bf16[1024,128]{1,0:T(8,128)(2,1)} %bitcast.64, bf16[4,128,512]{2,1,0:T(8,128)(2,1)} %all_gather.26.w1_ref, ...), custom_call_target="tpu_custom_call" | custom-call | flops 5000000000 | bytes 4000000 | tf_op jit(solution)/shard_map/back_chain/pallas_call | solution.py:373
  129.4 26.4 %exchange_2.1 = (bf16[4,1024,128]{2,1,0:T(8,128)(2,1)}, f32[4,32,512]{2,1,0:T(8,128)}, f32[4,128,128]{2,1,0:T(8,128)}) custom-call(bf16[1024,128]{1,0:T(8,128)(2,1)} %get-tuple-element.34.refs_0_, f32[4,32,512]{2,1,0:T(8,128)} %bitcast.56, f32[4,128,128]{2,1,0:T(8,128)} %bitcast.57), custom_call_target="tpu_custom_call" | custom-call | tf_op jit(solution)/shard_map/exchange_2/pallas_call | solution.py:131
  155.8 1.0 reduce_sum.47
  156.8 1.0 reduce_sum.45
  157.8 2.1 multiply_reduce_fusion
  159.8 2.1 multiply_reduce_fusion.1
  163.2 0.0 copy-start.2
  163.2 0.0 copy-start.4
  163.2 0.0 copy-start.5
  163.3 25.3 %add_rows.1 = (f32[30528,128]{1,0:T(8,128)}, f32[8,128]{1,0:T(8,128)}) custom-call(s32[1]{0:T(128)} %bitcast.1.me_ref, s32[4096]{0:T(1024)} %bitcast.65, bf16[4096,128]{1,0:T(8,128)(2,1)} %bitcast.63, f32[1920,128]{1,0:T(8,128)} %head_pass2.1.de_ref, f32[30528,128]{1,0:T(8,128)} %g_hbm.1), custom_call_target="tpu_custom_call" | custom-call | flops 10000000000 | bytes 32000000 | tf_op jit(solution)/shard_map/add_rows/pallas_call | solution.py:431
  188.5 0.0 copy-start.3
  188.5 0.0 copy-start.6
  188.6 0.0 copy-start.7
  188.6 1.4 broadcast_add_fusion.refs_0_
  189.9 11.5 %exchange_3.1 = (f32[16,8,128]{2,1,0:T(8,128)}, f32[4,32,512]{2,1,0:T(8,128)}, f32[4,128,128]{2,1,0:T(8,128)}) custom-call(f32[8,128]{1,0:T(8,128)} %broadcast_add_fusion.refs_0_, f32[32,512]{1,0:T(8,128)} %get-tuple-element.61.refs_1_, f32[128,128]{1,0:T(8,128)} %get-tuple-element.59.refs_2_), custom_call_target="tpu_custom_call" | custom-call | tf_op jit(solution)/shard_map/exchange_3/pallas_call | solution.py:131
  201.4 0.0 copy-start.8
  201.5 1.5 slice_reduce_fusion.1
  203.7 1.0 broadcast_multiply_fusion
  204.7 1.0 fusion.20
  205.7 6.8 %all_gather.31.w2_ref = bf16[4,512,128]{2,1,0:T(8,128)(2,1)} all-gather(bf16[1,512,128]{2,1,0:T(8,128)(2,1)S(1)} %get-tuple-element.50), channel_id=1, replica_groups=mesh['data'=4,'stage'=4] {'stage'}, dimensions={0}, use_global_device_ids=true | all-gather | bytes 655360 | tf_op jit(solution)/shard_map/all_gather | solution.py:562
  212.6 1.0 fusion.23
  213.6 7.2 %all_gather.30.w1_ref = bf16[4,128,512]{2,1,0:T(8,128)(2,1)} all-gather(bf16[1,128,512]{2,1,0:T(8,128)(2,1)S(1)} %get-tuple-element.54), channel_id=1, replica_groups=mesh['data'=4,'stage'=4] {'stage'}, dimensions={0}, use_global_device_ids=true | all-gather | bytes 655360 | tf_op jit(solution)/shard_map/all_gather | solution.py:561
  220.8 46.0 %adam_embed.1 = (f32[30528,128]{1,0:T(8,128)}, f32[30528,128]{1,0:T(8,128)}, f32[30528,128]{1,0:T(8,128)}) custom-call(f32[1]{0:T(128)} %bitcast.20.c_ref, f32[30528,128]{1,0:T(8,128)} %w_ref.1, f32[30528,128]{1,0:T(8,128)} %m_ref.1, f32[30528,128]{1,0:T(8,128)} %v_ref.1, f32[30528,128]{1,0:T(8,128)} %get-tuple-element.46.b_ref, ...), custom_call_target="tpu_custom_call" | custom-call | flops 20000000000 | bytes 125000000 | tf_op jit(solution)/shard_map/adam_embed/pallas_call | solution.py:463
  266.8 49.1 %forward.1.half_ref = bf16[8192,128]{1,0:T(8,128)(2,1)} custom-call(s32[8192]{0:T(1024)} %bitcast.59, f32[30528,128]{1,0:T(8,128)} %get-tuple-element.78.table_hbm, bf16[4,128,512]{2,1,0:T(8,128)(2,1)} %all_gather.30.w1_ref, bf16[4,512,128]{2,1,0:T(8,128)(2,1)} %all_gather.31.w2_ref), custom_call_target="tpu_custom_call" | custom-call | tf_op jit(solution)/shard_map/forward/pallas_call | solution.py:504
  316.0 7.7 %swap_4.1 = bf16[2,8192,128]{2,1,0:T(8,128)(2,1)} custom-call(bf16[8192,128]{1,0:T(8,128)(2,1)} %forward.1.half_ref), custom_call_target="tpu_custom_call" | custom-call | tf_op jit(solution)/shard_map/swap_4/pallas_call | solution.py:204
  323.7 0.0 copy-start.1
  323.7 4.6 %copy.32 = bf16[16,1024,128]{2,1,0:T(8,128)(2,1)} copy(bf16[16,1024,128]{2,1,0:T(8,128)(2,1)} %bitcast.53) | data formatting | bytes 8388608
  (13 shorter events, 0.1 us)
Async XLA Ops:
  7.2 89.6 %copy-start = (s32[16,1024]{1,0:T(8,128)S(1)}, s32[16,1024]{1,0:T(8,128)}, u32[]{:S(2)}) copy-start(s32[16,1024]{1,0:T(8,128)} %param.32) | copy-start | bytes 196612
  7.2 69.5 %all-gather.6.cloned.1.call-start = ((), (), s32[]{:S(2)}) async-start(), calls=%async_computation.1 | async-start | bytes 1114112 | tf_op jit(solution)/shard_map/all_gather | solution.py:531
  17.2 97.8 %all-gather.4.cloned.1.call-start = ((), (), s32[]{:S(2)}) async-start(), calls=%async_computation | async-start | bytes 1310720 | tf_op jit(solution)/shard_map/all_gather | solution.py:532
  18.0 202.8 %all-gather.8.cloned.1.call-start = ((), (), s32[]{:S(2)}) async-start(), calls=%async_computation.2 | async-start | bytes 16711680 | tf_op jit(solution)/shard_map/all_gather | solution.py:543
  163.2 41.5 %copy-start.2 = (f32[1,512,128]{2,1,0:T(8,128)S(1)}, f32[1,512,128]{2,1,0:T(8,128)}, u32[]{:S(2)}) copy-start(f32[1,512,128]{2,1,0:T(8,128)} %param.18) | copy-start | bytes 786436
  163.2 41.5 %copy-start.4 = (f32[1,512,128]{2,1,0:T(8,128)S(1)}, f32[1,512,128]{2,1,0:T(8,128)}, u32[]{:S(2)}) copy-start(f32[1,512,128]{2,1,0:T(8,128)} %param.20) | copy-start | bytes 786436
  163.2 41.5 %copy-start.5 = (f32[1,512,128]{2,1,0:T(8,128)S(1)}, f32[1,512,128]{2,1,0:T(8,128)}, u32[]{:S(2)}) copy-start(f32[1,512,128]{2,1,0:T(8,128)} %param.22) | copy-start | bytes 786436
  188.5 24.0 %copy-start.3 = (f32[1,128,512]{2,1,0:T(8,128)S(1)}, f32[1,128,512]{2,1,0:T(8,128)}, u32[]{:S(2)}) copy-start(f32[1,128,512]{2,1,0:T(8,128)} %param.17) | copy-start | bytes 786436
  188.5 24.0 %copy-start.6 = (f32[1,128,512]{2,1,0:T(8,128)S(1)}, f32[1,128,512]{2,1,0:T(8,128)}, u32[]{:S(2)}) copy-start(f32[1,128,512]{2,1,0:T(8,128)} %param.19) | copy-start | bytes 786436
  188.6 24.0 %copy-start.7 = (f32[1,128,512]{2,1,0:T(8,128)S(1)}, f32[1,128,512]{2,1,0:T(8,128)}, u32[]{:S(2)}) copy-start(f32[1,128,512]{2,1,0:T(8,128)} %param.21) | copy-start | bytes 786436
  201.4 11.1 %copy-start.8 = (f32[4,32,512]{2,1,0:T(8,128)S(1)}, f32[4,32,512]{2,1,0:T(8,128)}, u32[]{:S(2)}) copy-start(f32[4,32,512]{2,1,0:T(8,128)} %get-tuple-element.44) | copy-start | bytes 786436
  323.7 4.7 %copy-start.1 = (s32[16,1024]{1,0:T(8,128)S(1)}, s32[16,1024]{1,0:T(8,128)}, u32[]{:S(2)}) copy-start(s32[16,1024]{1,0:T(8,128)} %param.32) | copy-start | bytes 196612
Sparse Core Ops, SparseCore 0:
  17.3 26.5 all-gather.5
  45.5 14.6 all-gather.3
  96.2 86.5 all-gather.7
